TPU v7x, 128 devices: a whole 4x4x4 slice. The times are simulated.
128 devices in a mesh: ep: 8 (over x, core), fsdp: 16 (over z, y).
Axes of the slice: x: 4, y: 4, z: 4, core: 2. Of those that a mesh axis runs over, the one named last changes fastest.
Arguments:
- master_gate: float32 [128, 2048, 768], P('ep', 'fsdp'), may hold values from -0.1875 to 0.1875
- master_up: float32 [128, 2048, 768], P('ep', 'fsdp'), may hold values from -0.1875 to 0.1875
- router_weight: float32 [2048, 128], P('fsdp', 'ep'), may hold values from -0.125 to 0.125
- router_gain: float32 [2048], P('fsdp'), may hold values from 0.25 to 1.75
Outputs:
- final_gate: bfloat16 [128, 2048, 768], P(('ep', 'fsdp'))
- final_up: bfloat16 [128, 2048, 768], P(('ep', 'fsdp'))
- scale_gate: float32 [128, 768], P(('ep', 'fsdp'))
- scale_up: float32 [128, 768], P(('ep', 'fsdp'))
- serve_router: bfloat16 [2048, 128], replicated
All inputs are finite; a program needn't handle non-finite values.
Results may differ from a plain program's by a relative error of at most 0.001.
Values may be sent and summed in bfloat16 or wider, within the bound.
A program may use at most 128 MiB of HBM per device.

v0:
```python
import jax
import jax.numpy as jnp
from jax import lax
from jax.sharding import Mesh
from jax.sharding import PartitionSpec as P

EP = ("ep_0", "ep_1")
EP_FSDP = ("ep_0", "ep_1", "fsdp")


def copy_for_each(value, axis):
    devices = lax.axis_size(axis)
    return lax.all_to_all(
        jnp.broadcast_to(value[None], (devices, *value.shape)), axis, 0, 0, tiled=True
    )


def taken_together(value, axis):
    return copy_for_each(value, axis).sum(axis=0)


def in_one(arrays, axis):
    ends = [0]
    for a in arrays:
        ends.append(ends[-1] + a.size)
    so_far = taken_together(jnp.concatenate([a.ravel() for a in arrays]), axis)
    return tuple((so_far[b:e].reshape(a.shape) for a, b, e in zip(arrays, ends, ends[1:])))


def sent_together(arrays, axis, split_dim, concat_dim, along):
    ends, at = ([], 0)
    for a in arrays[:-1]:
        at += a.shape[along]
        ends.append(at)
    both = jnp.concatenate(arrays, axis=along)
    return tuple(
        jnp.split(
            lax.all_to_all(both, axis, split_axis=split_dim, concat_axis=concat_dim, tiled=True),
            ends,
            axis=along,
        )
    )


def joined_along(parts, dim):
    dims = list(parts.shape[1:])
    dims[dim] *= parts.shape[0]
    return jnp.moveaxis(parts, 0, dim).reshape(dims)


def gather_directly(value, axis, dim):
    return joined_along(copy_for_each(value, axis), dim)


def gather_in_order(value, axes, sequence):
    parts = value[None]
    for k in sequence:
        parts = lax.all_gather(parts, axes[k], axis=0, tiled=True)
    block = [lax.axis_size(axes[k]) for k in reversed(sequence)]
    parts = parts.reshape(*block, *value.shape)
    turned = sorted(range(len(sequence)), key=lambda place: sequence[len(sequence) - 1 - place])
    return parts.transpose(*turned, *range(len(sequence), parts.ndim)).reshape(-1, *value.shape)


def gather_axes(value, axes, sequence, dim):
    return joined_along(gather_in_order(value, axes, sequence), dim)


def body(master_gate, master_up, router_weight, router_gain):
    total_gate, total_up = in_one(
        (jnp.sum(master_gate * master_gate, axis=1), jnp.sum(master_up * master_up, axis=1)), "fsdp"
    )
    scale_gate = jnp.sqrt(total_gate)
    scale_up = jnp.sqrt(total_up)
    narrow_gate, narrow_up = (
        (master_gate / jnp.expand_dims(scale_gate, 1)).astype(jnp.bfloat16),
        (master_up / jnp.expand_dims(scale_up, 1)).astype(jnp.bfloat16),
    )
    final_gate, final_up = sent_together((narrow_gate, narrow_up), "fsdp", 0, 1, 2)
    scale_gate = lax.dynamic_slice_in_dim(
        scale_gate, lax.axis_index("fsdp") * final_gate.shape[0], final_gate.shape[0], axis=0
    )
    scale_up = lax.dynamic_slice_in_dim(
        scale_up, lax.axis_index("fsdp") * final_up.shape[0], final_up.shape[0], axis=0
    )
    part_router = (router_weight * router_gain[:, None]).astype(jnp.bfloat16)
    row_router = gather_directly(part_router, "fsdp", 0)
    serve_router = gather_axes(row_router, ("ep_0", "ep_1"), (0, 1), 1)
    return (final_gate, final_up, scale_gate, scale_up, serve_router)


def solution(mesh):
    finer = Mesh(mesh.devices.reshape(4, 2, mesh.shape["fsdp"]), ("ep_0", "ep_1", "fsdp"))
    return jax.shard_map(
        body,
        mesh=finer,
        in_specs=(P(EP, "fsdp", None), P(EP, "fsdp", None), P("fsdp", EP), P("fsdp")),
        out_specs=(
            P(EP_FSDP, None, None),
            P(EP_FSDP, None, None),
            P(EP_FSDP, None),
            P(EP_FSDP, None),
            P(),
        ),
        check_vma=False,
    )
```

profile of v0, /device:TPU:0, one launch (start us, length us, event | category | flops | bytes accessed | tf_op | source)
XLA Modules:
  0.0 161.2 jit_solution(398515752994868322)
XLA Ops:
  0.6 3.3 %multiply_reduce_fusion.1 = f32[16,768]{1,0:T(8,128)S(1)} fusion(f32[16,128,768]{2,1,0:T(8,128)} %param.4), kind=kLoop, calls=%fused_computation.4 | loop fusion | flops 3133440 | bytes 6340608 | tf_op jit(solution)/shard_map/reduce_sum | solution.py:71
  4.0 0.0 copy-start
  4.0 0.0 copy-start.1
  4.0 3.3 %multiply_reduce_fusion = f32[16,768]{1,0:T(8,128)S(1)} fusion(f32[16,128,768]{2,1,0:T(8,128)} %param.5), kind=kLoop, calls=%fused_computation.3 | loop fusion | flops 3133440 | bytes 6340608 | tf_op jit(solution)/shard_map/reduce_sum | solution.py:71
  7.4 2.4 %broadcast_in_dim.4 = f32[16,1,24576]{2,1,0:T(1,128)} broadcast(f32[24576]{0:T(1024)S(1)} %pad_maximum_fusion.1), dimensions={2} | broadcast | bytes 1671168 | tf_op jit(solution)/shard_map/broadcast_in_dim | solution.py:14
  9.7 8.2 %all-to-all-start = ((f32[16,1,24576]{2,1,0:T(1,128)}), f32[16,1,24576]{2,1,0:T(1,128)S(1)}, u32[]{:S(2)}, u32[]{:S(2)}) async-start(f32[16,1,24576]{2,1,0:T(1,128)} %broadcast_in_dim.4), calls=%async_computation | async-start | bytes 3145728 | tf_op jit(solution)/shard_map/all_to_all | solution.py:13
  17.9 0.0 copy-done
  17.9 0.0 copy-done.1
  17.9 24.5 %all-to-all-done = f32[16,1,24576]{2,1,0:T(1,128)S(1)} async-done(((f32[16,1,24576]{2,1,0:T(1,128)}), f32[16,1,24576]{2,1,0:T(1,128)S(1)}, u32[]{:S(2)}, u32[]{:S(2)}) %all-to-all-start) | async-done | bytes 1572896 | tf_op jit(solution)/shard_map/all_to_all | solution.py:13
  42.4 0.6 broadcast_in_dim.5
  43.1 3.5 %all-to-all-start.2 = ((bf16[16,128,16]{1,2,0:T(8,128)(2,1)}), bf16[16,128,16]{1,2,0:T(8,128)(2,1)S(1)}, u32[]{:S(2)}, u32[]{:S(2)}) async-start(bf16[16,128,16]{1,2,0:T(8,128)(2,1)} %broadcast_in_dim.5), calls=%async_computation.2 | async-start | bytes 131072 | tf_op jit(solution)/shard_map/all_to_all | solution.py:13
  46.6 1.0 reduce_sum.29
  47.7 5.3 %divide_convert_fusion = (bf16[16,128,768]{2,1,0:T(8,128)(2,1)S(1)}, bf16[16,128,768]{2,1,0:T(8,128)(2,1)S(1)}) fusion(f32[16,128,768]{2,1,0:T(8,128)} %param.5, f32[16,768]{1,0:T(8,128)S(1)} %sqrt.15, f32[16,128,768]{2,1,0:T(8,128)} %param.4, f32[16,768]{1,0:T(8,128)S(1)} %sqrt.13), kind=kLoop, calls=%fused_computation.1 | loop fusion | flops 6291456 | bytes 18972672 | tf_op jit(solution)/shard_map/convert_element_type | solution.py:77
  53.0 3.2 %pad_maximum_fusion = bf16[16,128,1536]{2,1,0:T(8,128)(2,1)} fusion(bf16[16,128,768]{2,1,0:T(8,128)(2,1)S(1)} %get-tuple-element.39, bf16[16,128,768]{2,1,0:T(8,128)(2,1)S(1)} %get-tuple-element.40), kind=kLoop, calls=%fused_computation | loop fusion | flops 12582912 | bytes 12582912 | tf_op jit(solution)/shard_map/concatenate | solution.py:35
  56.2 0.0 all-to-all-done.2
  56.2 7.2 %all-to-all-start.1 = ((bf16[16,128,1536]{2,1,0:T(8,128)(2,1)}), bf16[16,128,1536]{2,1,0:T(8,128)(2,1)}, u32[]{:S(2)}, u32[]{:S(2)}) async-start(bf16[16,128,1536]{2,1,0:T(8,128)(2,1)} %pad_maximum_fusion), calls=%async_computation.1 | async-start | bytes 12582912 | tf_op jit(solution)/shard_map/all_to_all | solution.py:38
  63.5 12.7 %all_gather.6 = bf16[4,2048,16]{1,2,0:T(8,128)(2,1)S(1)} all-gather(bf16[1,2048,16]{1,2,0:T(8,128)(2,1)S(1)} %broadcast_in_dim_reshape.3), channel_id=1, replica_groups=mesh['ep_0'=4,'ep_1'=2,'fsdp'=16] {'ep_0'}, dimensions={0}, use_global_device_ids=true | all-gather | bytes 327680 | tf_op jit(solution)/shard_map/all_gather | solution.py:58
  76.2 2.2 %all_gather.7 = bf16[8,2048,16]{1,2,0:T(8,128)(2,1)S(1)} all-gather(bf16[4,2048,16]{1,2,0:T(8,128)(2,1)S(1)} %all_gather.6), channel_id=1, replica_groups=mesh['ep_0'=4,'ep_1'=2,'fsdp'=16] {'ep_1'}, dimensions={0}, use_global_device_ids=true | all-gather | bytes 786432 | tf_op jit(solution)/shard_map/all_gather | solution.py:58
  78.4 1.0 copy.24
  79.4 0.6 constant_dynamic-slice_fusion
  80.0 75.3 %all-to-all-done.1 = bf16[16,128,1536]{2,1,0:T(8,128)(2,1)} async-done(((bf16[16,128,1536]{2,1,0:T(8,128)(2,1)}), bf16[16,128,1536]{2,1,0:T(8,128)(2,1)}, u32[]{:S(2)}, u32[]{:S(2)}) %all-to-all-start.1) | async-done | bytes 6291488 | tf_op jit(solution)/shard_map/all_to_all | solution.py:38
  155.2 5.9 %fusion = (bf16[1,2048,768]{2,1,0:T(8,128)(2,1)}, bf16[1,2048,768]{2,1,0:T(8,128)(2,1)}) fusion(bf16[1,2048,1536]{2,1,0:T(8,128)(2,1)} %bitcast), kind=kLoop, calls=%fused_computation.11 | loop fusion | bytes 12582912 | tf_op jit(solution)/shard_map/split | solution.py:37
  (10 shorter events, 0.2 us)
Async XLA Ops:
  4.0 13.9 %copy-start = (f32[128,16]{0,1:T(8,128)S(1)}, f32[128,16]{0,1:T(8,128)}, u32[]{:S(2)}) copy-start(f32[128,16]{0,1:T(8,128)} %param.6) | copy-start | bytes 24580
  4.0 13.9 %copy-start.1 = (f32[128]{0:T(128)S(1)}, f32[128]{0:T(128)}, u32[]{:S(2)}) copy-start(f32[128]{0:T(128)} %param.7) | copy-start | bytes 1540
  9.7 32.7 %all-to-all-start = ((f32[16,1,24576]{2,1,0:T(1,128)}), f32[16,1,24576]{2,1,0:T(1,128)S(1)}, u32[]{:S(2)}, u32[]{:S(2)}) async-start(f32[16,1,24576]{2,1,0:T(1,128)} %broadcast_in_dim.4), calls=%async_computation | async-start | bytes 3145728 | tf_op jit(solution)/shard_map/all_to_all | solution.py:13
  43.1 13.2 %all-to-all-start.2 = ((bf16[16,128,16]{1,2,0:T(8,128)(2,1)}), bf16[16,128,16]{1,2,0:T(8,128)(2,1)S(1)}, u32[]{:S(2)}, u32[]{:S(2)}) async-start(bf16[16,128,16]{1,2,0:T(8,128)(2,1)} %broadcast_in_dim.5), calls=%async_computation.2 | async-start | bytes 131072 | tf_op jit(solution)/shard_map/all_to_all | solution.py:13
  56.2 99.0 %all-to-all-start.1 = ((bf16[16,128,1536]{2,1,0:T(8,128)(2,1)}), bf16[16,128,1536]{2,1,0:T(8,128)(2,1)}, u32[]{:S(2)}, u32[]{:S(2)}) async-start(bf16[16,128,1536]{2,1,0:T(8,128)(2,1)} %pad_maximum_fusion), calls=%async_computation.1 | async-start | bytes 12582912 | tf_op jit(solution)/shard_map/all_to_all | solution.py:38
where the time goes:
time: 162 us; the launch traced here: 161 us
  waiting for transfers between devices  99.7 us (62%)
  starting transfers between devices  18.9 us (12%)
  other arithmetic  16.2 us (10%)
  blocking collectives  14.8 us (9%)
  local copies, waits for them, and re-layouts  10.7 us (7%)
    all_to_all x1, waiting for transfers between devices, sent_together(): lax.all_to_all(both, axis, split_axis=split_dim, concat_axis=concat_dim,...  75.3 us
    all_to_all x2, waiting for transfers between devices, copy_for_each(): lax.all_to_all(jnp.broadcast_to(value[None], (devices, *value.shape)), ax...  24.5 us
    all_gather x2, blocking collectives, gather_in_order(): parts = lax.all_gather(parts, axes[k], axis=0, tiled=True)  14.8 us
    all_to_all x2, starting transfers between devices, copy_for_each(): lax.all_to_all(jnp.broadcast_to(value[None], (devices, *value.shape)), ax...  11.7 us
    all_to_all x1, starting transfers between devices, sent_together(): lax.all_to_all(both, axis, split_axis=split_dim, concat_axis=concat_dim,...  7.2 us
    split x1, local copies, waits for them, and re-layouts, sent_together(): jnp.split(lax.all_to_all(both, axis, split_axis=split_dim, concat_axis=co...  5.95 us
    convert_element_type x1, other arithmetic, body(): (master_up / jnp.expand_dims(scale_up, 1)).astype(jnp.bfloat16)  5.31 us
    reduce_sum x1, other arithmetic, body(): jnp.sum(master_gate * master_gate, axis=1)  3.33 us
  transfers between devices with their start and end apart: 3, of which 2 were waited for; matrix products, arithmetic and copies ran while one was open for 7% of the time, Pallas kernels for 0%

commit v1 on v0

--- a/solution.py
+++ b/solution.py
@@ -3,9 +3,18 @@
 from jax import lax
 from jax.sharding import Mesh
 from jax.sharding import PartitionSpec as P
+from jax.lax import all_to_all, axis_size
 
 EP = ("ep_0", "ep_1")
 EP_FSDP = ("ep_0", "ep_1", "fsdp")
+
+
+def replace_plate(array_axis, slab_in, peer_axis):
+    last = axis_size(peer_axis)
+    y = jnp.stack([slab_in] * last, 0)
+    r1 = all_to_all(y, peer_axis, 0, 0)
+    even = jnp.concatenate(r1, array_axis)
+    return even
 
 
 def copy_for_each(value, axis):
@@ -55,7 +64,7 @@
 def gather_in_order(value, axes, sequence):
     parts = value[None]
     for k in sequence:
-        parts = lax.all_gather(parts, axes[k], axis=0, tiled=True)
+        parts = replace_plate(0, parts, axes[k])
     block = [lax.axis_size(axes[k]) for k in reversed(sequence)]
     parts = parts.reshape(*block, *value.shape)
     turned = sorted(range(len(sequence)), key=lambda place: sequence[len(sequence) - 1 - place])

time: 162 us -> 180 us (1.11)
  waiting for transfers between devices: 99.7 us -> 125 us
  blocking collectives: 14.8 us -> 0 us
  starting transfers between devices: 18.9 us -> 25.3 us
  local copies, waits for them, and re-layouts: 10.7 us -> 12.5 us
    all_to_all x1, waiting for transfers between devices: 75.3 us -> 95.3 us  [sent_together(): lax.all_to_all(both, axis, split_axis=split_dim, concat_axis=concat_dim,...]
    all_gather x2 -> x0, blocking collectives: 14.8 us -> none  [gather_in_order(): parts = lax.all_gather(parts, axes[k], axis=0, tiled=True)]
    all_to_all x0 -> x2, starting transfers between devices: none -> 7.78 us  [replace_plate(): r1 = all_to_all(y, peer_axis, 0, 0)]
    all_to_all x0 -> x2, waiting for transfers between devices: none -> 6.67 us  [replace_plate(): r1 = all_to_all(y, peer_axis, 0, 0)]
    reduce_sum x1, other arithmetic: 3.33 us -> 0.54 us  [body(): jnp.sum(master_up * master_up, axis=1)]
    all_to_all x1, starting transfers between devices: 7.2 us -> 4.65 us  [sent_together(): lax.all_to_all(both, axis, split_axis=split_dim, concat_axis=concat_dim,...]
  transfers between devices with their start and end apart: 3 -> 5, of which waited for: 2 -> 4; matrix products, arithmetic and copies ran while one was open for 7% -> 9% of each run, Pallas kernels for 0% -> 0%
where the time goes in v1:
time: 180 us; the launch traced here: 179 us
  waiting for transfers between devices  125 us (69%)
  starting transfers between devices  25.3 us (14%)
  other arithmetic  15.1 us (8%)
  local copies, waits for them, and re-layouts  12.5 us (7%)
    all_to_all x1, waiting for transfers between devices, sent_together(): lax.all_to_all(both, axis, split_axis=split_dim, concat_axis=concat_dim,...  95.3 us
    all_to_all x2, waiting for transfers between devices, copy_for_each(): lax.all_to_all(jnp.broadcast_to(value[None], (devices, *value.shape)), ax...  23.4 us
    all_to_all x2, starting transfers between devices, copy_for_each(): lax.all_to_all(jnp.broadcast_to(value[None], (devices, *value.shape)), ax...  12.9 us
    all_to_all x2, starting transfers between devices, replace_plate(): r1 = all_to_all(y, peer_axis, 0, 0)  7.78 us
    all_to_all x2, waiting for transfers between devices, replace_plate(): r1 = all_to_all(y, peer_axis, 0, 0)  6.67 us
    split x1, local copies, waits for them, and re-layouts, sent_together(): jnp.split(lax.all_to_all(both, axis, split_axis=split_dim, concat_axis=co...  5.95 us
    convert_element_type x1, other arithmetic, body(): (master_up / jnp.expand_dims(scale_up, 1)).astype(jnp.bfloat16)  5.31 us
    all_to_all x1, starting transfers between devices, sent_together(): lax.all_to_all(both, axis, split_axis=split_dim, concat_axis=concat_dim,...  4.65 us
  transfers between devices with their start and end apart: 5, of which 4 were waited for; matrix products, arithmetic and copies ran while one was open for 9% of the time, Pallas kernels for 0%

profile of v1, /device:TPU:0, one launch (start us, length us, event | category | flops | bytes accessed | tf_op | source)
XLA Modules:
  0.0 179.0 jit_solution(4801421026315068205)
XLA Ops:
  0.6 0.7 multiply_convert_fusion
  1.3 0.6 broadcast_in_dim.5
  2.0 8.2 %all-to-all-start.2 = ((bf16[16,128,16]{1,2,0:T(8,128)(2,1)}), bf16[16,128,16]{1,2,0:T(8,128)(2,1)S(1)}, u32[]{:S(2)}, u32[]{:S(2)}) async-start(bf16[16,128,16]{1,2,0:T(8,128)(2,1)} %broadcast_in_dim.5), calls=%async_computation.2 | async-start | bytes 131072 | tf_op jit(solution)/shard_map/all_to_all | solution.py:22
  10.1 0.0 copy-start
  10.2 3.5 %multiply_reduce_fusion.1 = f32[16,768]{1,0:T(8,128)S(1)} fusion(f32[16,128,768]{2,1,0:T(8,128)} %param.4), kind=kLoop, calls=%fused_computation.4 | loop fusion | flops 3133440 | bytes 6340608 | tf_op jit(solution)/shard_map/reduce_sum | solution.py:80
  13.6 1.1 copy-done
  14.7 0.5 multiply_reduce_fusion
  15.3 2.5 %all-to-all-done.2 = bf16[16,128,16]{1,2,0:T(8,128)(2,1)S(1)} async-done(((bf16[16,128,16]{1,2,0:T(8,128)(2,1)}), bf16[16,128,16]{1,2,0:T(8,128)(2,1)S(1)}, u32[]{:S(2)}, u32[]{:S(2)}) %all-to-all-start.2) | async-done | bytes 65568 | tf_op jit(solution)/shard_map/all_to_all | solution.py:22
  17.8 0.7 stack.6
  18.5 4.3 %all-to-all-start.3 = ((bf16[4,1,2048,16]{2,3,1,0:T(8,128)(2,1)}), bf16[4,1,2048,16]{2,3,1,0:T(8,128)(2,1)S(1)}, u32[]{:S(2)}, u32[]{:S(2)}) async-start(bf16[4,1,2048,16]{2,3,1,0:T(8,128)(2,1)} %stack.6), calls=%async_computation.3 | async-start | bytes 524288 | tf_op jit(solution)/shard_map/all_to_all | solution.py:15
  22.8 6.7 %all-to-all-done.3 = bf16[4,1,2048,16]{2,3,1,0:T(8,128)(2,1)S(1)} async-done(((bf16[4,1,2048,16]{2,3,1,0:T(8,128)(2,1)}), bf16[4,1,2048,16]{2,3,1,0:T(8,128)(2,1)S(1)}, u32[]{:S(2)}, u32[]{:S(2)}) %all-to-all-start.3) | async-done | bytes 262176 | tf_op jit(solution)/shard_map/all_to_all | solution.py:15
  29.5 2.4 %broadcast_in_dim.4 = f32[16,1,24576]{2,1,0:T(1,128)} broadcast(f32[24576]{0:T(1024)S(1)} %pad_maximum_fusion.2), dimensions={2} | broadcast | bytes 1671168 | tf_op jit(solution)/shard_map/broadcast_in_dim | solution.py:23
  31.9 4.7 %all-to-all-start = ((f32[16,1,24576]{2,1,0:T(1,128)}), f32[16,1,24576]{2,1,0:T(1,128)S(1)}, u32[]{:S(2)}, u32[]{:S(2)}) async-start(f32[16,1,24576]{2,1,0:T(1,128)} %broadcast_in_dim.4), calls=%async_computation | async-start | bytes 3145728 | tf_op jit(solution)/shard_map/all_to_all | solution.py:22
  36.6 0.8 pad_maximum_fusion.1
  37.4 20.9 %all-to-all-done = f32[16,1,24576]{2,1,0:T(1,128)S(1)} async-done(((f32[16,1,24576]{2,1,0:T(1,128)}), f32[16,1,24576]{2,1,0:T(1,128)S(1)}, u32[]{:S(2)}, u32[]{:S(2)}) %all-to-all-start) | async-done | bytes 1572896 | tf_op jit(solution)/shard_map/all_to_all | solution.py:22
  58.3 3.5 %all-to-all-start.4 = ((bf16[2,4,2048,16]{2,3,1,0:T(8,128)(2,1)}), bf16[2,4,2048,16]{2,3,1,0:T(8,128)(2,1)S(1)}, u32[]{:S(2)}, u32[]{:S(2)}) async-start(bf16[2,4,2048,16]{2,3,1,0:T(8,128)(2,1)} %pad_maximum_fusion.1), calls=%async_computation.4 | async-start | bytes 1048576 | tf_op jit(solution)/shard_map/all_to_all | solution.py:15
  61.8 1.0 reduce_sum.29
  62.9 5.3 %divide_convert_fusion = (bf16[16,128,768]{2,1,0:T(8,128)(2,1)S(1)}, bf16[16,128,768]{2,1,0:T(8,128)(2,1)S(1)}) fusion(f32[16,128,768]{2,1,0:T(8,128)} %param.5, f32[16,768]{1,0:T(8,128)S(1)} %sqrt.15, f32[16,128,768]{2,1,0:T(8,128)} %param.4, f32[16,768]{1,0:T(8,128)S(1)} %sqrt.13), kind=kLoop, calls=%fused_computation.1 | loop fusion | flops 6291456 | bytes 18972672 | tf_op jit(solution)/shard_map/convert_element_type | solution.py:86
  68.3 3.2 %pad_maximum_fusion = bf16[16,128,1536]{2,1,0:T(8,128)(2,1)} fusion(bf16[16,128,768]{2,1,0:T(8,128)(2,1)S(1)} %get-tuple-element.39, bf16[16,128,768]{2,1,0:T(8,128)(2,1)S(1)} %get-tuple-element.40), kind=kLoop, calls=%fused_computation | loop fusion | flops 12582912 | bytes 12582912 | tf_op jit(solution)/shard_map/concatenate | solution.py:44
  71.5 0.0 all-to-all-done.4
  71.5 4.6 %all-to-all-start.1 = ((bf16[16,128,1536]{2,1,0:T(8,128)(2,1)}), bf16[16,128,1536]{2,1,0:T(8,128)(2,1)}, u32[]{:S(2)}, u32[]{:S(2)}) async-start(bf16[16,128,1536]{2,1,0:T(8,128)(2,1)} %pad_maximum_fusion), calls=%async_computation.1 | async-start | bytes 12582912 | tf_op jit(solution)/shard_map/all_to_all | solution.py:47
  76.2 1.0 copy.24
  77.2 0.6 constant_dynamic-slice_fusion
  77.8 95.3 %all-to-all-done.1 = bf16[16,128,1536]{2,1,0:T(8,128)(2,1)} async-done(((bf16[16,128,1536]{2,1,0:T(8,128)(2,1)}), bf16[16,128,1536]{2,1,0:T(8,128)(2,1)}, u32[]{:S(2)}, u32[]{:S(2)}) %all-to-all-start.1) | async-done | bytes 6291488 | tf_op jit(solution)/shard_map/all_to_all | solution.py:47
  173.1 5.9 %fusion = (bf16[1,2048,768]{2,1,0:T(8,128)(2,1)}, bf16[1,2048,768]{2,1,0:T(8,128)(2,1)}) fusion(bf16[1,2048,1536]{2,1,0:T(8,128)(2,1)} %bitcast), kind=kLoop, calls=%fused_computation.13 | loop fusion | bytes 12582912 | tf_op jit(solution)/shard_map/split | solution.py:46
  (8 shorter events, 0.1 us)
Async XLA Ops:
  2.0 15.8 %all-to-all-start.2 = ((bf16[16,128,16]{1,2,0:T(8,128)(2,1)}), bf16[16,128,16]{1,2,0:T(8,128)(2,1)S(1)}, u32[]{:S(2)}, u32[]{:S(2)}) async-start(bf16[16,128,16]{1,2,0:T(8,128)(2,1)} %broadcast_in_dim.5), calls=%async_computation.2 | async-start | bytes 131072 | tf_op jit(solution)/shard_map/all_to_all | solution.py:22
  10.1 4.6 %copy-start = (f32[16,128,768]{2,1,0:T(8,128)S(1)}, f32[16,128,768]{2,1,0:T(8,128)}, u32[]{:S(2)}) copy-start(f32[16,128,768]{2,1,0:T(8,128)} %param.5) | copy-start | bytes 18874372
  18.5 11.0 %all-to-all-start.3 = ((bf16[4,1,2048,16]{2,3,1,0:T(8,128)(2,1)}), bf16[4,1,2048,16]{2,3,1,0:T(8,128)(2,1)S(1)}, u32[]{:S(2)}, u32[]{:S(2)}) async-start(bf16[4,1,2048,16]{2,3,1,0:T(8,128)(2,1)} %stack.6), calls=%async_computation.3 | async-start | bytes 524288 | tf_op jit(solution)/shard_map/all_to_all | solution.py:15
  31.9 26.5 %all-to-all-start = ((f32[16,1,24576]{2,1,0:T(1,128)}), f32[16,1,24576]{2,1,0:T(1,128)S(1)}, u32[]{:S(2)}, u32[]{:S(2)}) async-start(f32[16,1,24576]{2,1,0:T(1,128)} %broadcast_in_dim.4), calls=%async_computation | async-start | bytes 3145728 | tf_op jit(solution)/shard_map/all_to_all | solution.py:22
  58.3 13.1 %all-to-all-start.4 = ((bf16[2,4,2048,16]{2,3,1,0:T(8,128)(2,1)}), bf16[2,4,2048,16]{2,3,1,0:T(8,128)(2,1)S(1)}, u32[]{:S(2)}, u32[]{:S(2)}) async-start(bf16[2,4,2048,16]{2,3,1,0:T(8,128)(2,1)} %pad_maximum_fusion.1), calls=%async_computation.4 | async-start | bytes 1048576 | tf_op jit(solution)/shard_map/all_to_all | solution.py:15
  71.5 101.6 %all-to-all-start.1 = ((bf16[16,128,1536]{2,1,0:T(8,128)(2,1)}), bf16[16,128,1536]{2,1,0:T(8,128)(2,1)}, u32[]{:S(2)}, u32[]{:S(2)}) async-start(bf16[16,128,1536]{2,1,0:T(8,128)(2,1)} %pad_maximum_fusion), calls=%async_computation.1 | async-start | bytes 12582912 | tf_op jit(solution)/shard_map/all_to_all | solution.py:47
